TPU v7x, 32 devices: a whole 2x2x4 slice. The times are simulated.
32 devices in a mesh: seq: 8 (over z, x), feat: 4 (over y, core).
Axes of the slice: x: 2, y: 2, z: 4, core: 2. Of those that a mesh axis runs over, the one named last changes fastest.
Arguments:
- injection: bfloat16 [1024, 5120], P('seq', 'feat'), may hold values from -8 to 8
- warm_start: bfloat16 [1024, 5120], P('seq', 'feat'), may hold values from -12 to 12
- gain_in: float32 [5120], replicated, may hold values from 0.5 to 1.5
- gain_out: float32 [5120], replicated, may hold values from 0.5 to 1.5
- w_query: bfloat16 [5120, 5120], P(None, 'feat'), may hold values from -0.0848993624 to 0.0848993624
- w_key: bfloat16 [5120, 1024], P(None, 'feat'), may hold values from -0.0848993624 to 0.0848993624
- w_value: bfloat16 [5120, 1024], P(None, 'feat'), may hold values from -0.078125 to 0.078125
- w_out: bfloat16 [5120, 5120], P('feat'), may hold values from -0.078125 to 0.078125
Outputs:
- equilibrium: float32 [1024, 5120], P('seq', 'feat')
All inputs are finite; a program needn't handle non-finite values.
Results may differ from a plain program's by a relative error of at most 0.009.
Values may be sent and summed in bfloat16 or wider, within the bound.
A program may use at most 128 MiB of HBM per device.

v0:
```python
import functools
import math

import jax
import jax.numpy as jnp
from jax import lax
from jax.experimental import pallas as pl
from jax.experimental.pallas import tpu as pltpu
from jax.sharding import PartitionSpec as P

HEADS = 40
KV_HEADS = 8
HEAD_DIM = 128
ITERS = 4

EPS = 1e-06
LAMBDA = 0.03
CHUNKS = 5
HALVES = 2
MESH = pl.DeviceIdType.MESH
VMEM = pl.BlockSpec(memory_space=pltpu.VMEM)
ANY = pl.BlockSpec(memory_space=pl.ANY)


def remote(src, dst, send_sem, recv_sem, axis, target):
    return pltpu.make_async_remote_copy(
        src_ref=src, dst_ref=dst, send_sem=send_sem, recv_sem=recv_sem,
        device_id={axis: target}, device_id_type=MESH,
    )


def solve_values(rows, values):
    size = len(values)
    rows = [list(row) for row in rows]
    values = list(values)
    for pivot in range(size):
        for below in range(pivot + 1, size):
            ratio = rows[below][pivot] / rows[pivot][pivot]
            for at in range(pivot, size):
                rows[below][at] = rows[below][at] - ratio * rows[pivot][at]
            values[below] = values[below] - ratio * values[pivot]
    result = [None] * size
    for pivot in reversed(range(size)):
        running = values[pivot]
        for later in range(pivot + 1, size):
            running = running - rows[pivot][later] * result[later]
        result[pivot] = running / rows[pivot][pivot]
    return result


def whole_kernel(n, m, inj_hbm, warm_hbm, gain_in, gain_out, wq_hbm, wk_hbm, wv_hbm, wo_hbm, out,
                 tok, tok_inj, w_kv, w_q, w_o, inj, warm, images, residuals, held, proj, queries, kv,
                 acc, top, bias, attended, keep, near_out, near, outgoing, far, coef, gram,
                 scale_out, scale_in, mail_out, mail, wide_out, wide,
                 load_sem, feat_s, feat_r, inj_s, inj_r, up_s, up_r, side_s, side_r,
                 near_s, near_r, far_s, far_r, mail_s, mail_r, wide_s, wide_r):
    me = lax.axis_index("feat")
    side = lax.rem(me, 2)
    mine = lax.div(me, 2)
    partner = me + 1 - 2 * side
    lines = n // 2
    lined = [lax.rem(mine + d, lines) for d in range(lines)]
    before = [lax.rem(mine - d + lines, lines) for d in range(lines)]
    at_seq = lax.axis_index("seq")
    row_side = lax.rem(at_seq, 2)
    level = lax.div(at_seq, 2)
    levels = m // 2
    row_partner = at_seq + 1 - 2 * row_side

    toks, part = inj.shape
    width = n * part
    head_cols = w_q.shape[1]
    kv_cols = w_kv.shape[1] // 2
    kv_local = kv_cols // HEAD_DIM
    heads = head_cols // HEAD_DIM
    group = heads // kv_local
    span = part // CHUNKS
    half = toks // HALVES
    lanes = 128
    scale_all = float(toks * m * width)
    factor = math.log2(math.e) / math.sqrt(HEAD_DIM)
    f32, bf16 = jnp.float32, jnp.bfloat16

    loads = [
        pltpu.make_async_copy(inj_hbm, inj, load_sem.at[0]),
        pltpu.make_async_copy(warm_hbm, warm, load_sem.at[1]),
        pltpu.make_async_copy(wk_hbm, w_kv.at[:, pl.ds(0, kv_cols)], load_sem.at[2]),
        pltpu.make_async_copy(wv_hbm, w_kv.at[:, pl.ds(kv_cols, kv_cols)], load_sem.at[3]),
        pltpu.make_async_copy(wq_hbm, w_q, load_sem.at[4]),
        pltpu.make_async_copy(wo_hbm, w_o, load_sem.at[5]),
    ]
    for load in loads:
        load.start()

    barrier = pltpu.get_barrier_semaphore()
    for d in range(1, n):
        pl.semaphore_signal(barrier, inc=1, device_id={"feat": lax.rem(me + d, n)}, device_id_type=MESH)
    for d in range(1, m):
        pl.semaphore_signal(barrier, inc=1, device_id={"seq": lax.rem(at_seq + d, m)}, device_id_type=MESH)

    def columns(at, size):
        return pl.ds(pl.multiple_of(at * size, size), size)

    def blocks_of(ref_width):
        return ref_width // lanes

    def row_sums(partial):
        return jnp.broadcast_to(jnp.sum(partial.T, axis=0, keepdims=True), (8, toks))

    def by_token(total):
        scale = lax.rsqrt(total * (1.0 / width) + EPS)
        return jnp.broadcast_to(scale[:1], (lanes, toks)).T

    zero_tile = jnp.zeros((toks, lanes), f32)

    @pl.loop(0, blocks_of(part))
    def _(at):
        cols = columns(at, lanes)
        for j in range(ITERS):
            images[j, :, cols] = zero_tile
            residuals[j, :, cols] = zero_tile

    @pl.loop(0, blocks_of(head_cols + 2 * kv_cols))
    def _(at):
        cols = columns(at, lanes)
        for j in range(ITERS):
            proj[j, :, cols] = zero_tile

    for j in range(ITERS):
        coef[j] = jnp.full((8, lanes), 1.0 if j == 0 else 0.0, f32)
    for j in range(ITERS * ITERS):
        gram[j] = jnp.zeros((8, lanes), f32)
    scale_out[...] = jnp.ones((toks, lanes), f32)

    @pl.when(row_side == 0)
    def _():
        for slot in range(2):
            kv[slot, at_seq + 1] = jnp.zeros(kv.shape[2:], bf16)

    key_at = lax.broadcasted_iota(jnp.int32, (toks, 2 * toks), 1)
    query_at = lax.broadcasted_iota(jnp.int32, (toks, 2 * toks), 0) + row_side * toks
    bias[0] = jnp.where(key_at <= query_at, 0.0, -1e30).astype(f32)
    bias[1] = jnp.zeros((toks, 2 * toks), f32)

    loads[0].wait()
    loads[1].wait()

    def gather_copy(buffer, cols, sems, d):
        here = buffer.at[me, :, cols]
        target = partner if d == 0 else 2 * lined[d] + side
        return remote(here, here, sems[0], sems[1], "feat", target)

    def forward_copy(buffer, cols, sems, d):
        here = buffer.at[2 * before[d] + side, :, cols]
        return remote(here, here, sems[0], sems[1], "feat", partner)

    def gather_step(c, d):
        return gather_copy(tok, columns(c, span), (feat_s.at[c, d], feat_r.at[c, d]), d)

    def forward_step(c, d):
        at = lines - 1 + d
        return forward_copy(tok, columns(c, span), (feat_s.at[c, at], feat_r.at[c, at]), d)

    def inj_step(d):
        return gather_copy(tok_inj, pl.ds(0, part), (inj_s.at[d], inj_r.at[d]), d)

    def inj_forward(d):
        at = lines - 1 + d
        return forward_copy(tok_inj, pl.ds(0, part), (inj_s.at[at], inj_r.at[at]), d)

    def start_block(at, total):
        cols = columns(at, lanes)
        gain = gain_in[me, :, cols]
        base = inj[:, cols].astype(f32)
        first = warm[:, cols].astype(f32)
        out[:, cols] = first
        mixed = first + base
        tok[me, :, cols] = (mixed * gain).astype(bf16)
        tok_inj[me, :, cols] = (base * gain).astype(bf16)
        return total + mixed * mixed

    total = lax.fori_loop(0, blocks_of(part), start_block, zero_tile)
    mail_out[1] = row_sums(total)
    pl.semaphore_wait(barrier, n + m - 2)
    for c in range(CHUNKS):
        for d in range(1, lines):
            gather_step(c, d).start()
        gather_step(c, 0).start()
    for d in range(lines):
        inj_step(d).start()

    def feat_sum(which):
        copies = [
            remote(mail_out.at[which], mail.at[which, d], mail_s.at[which, d], mail_r.at[which, d],
                   "feat", lax.rem(me + d, n))
            for d in range(1, n)
        ]
        for copy in copies:
            copy.start()
        total = mail_out[which]
        for d, copy in enumerate(copies):
            copy.wait()
            total = total + mail[which, d + 1]
        return total

    def seq_sum(slot, value):
        wide_out[...] = value
        copies = [
            remote(wide_out, wide.at[slot, d], wide_s.at[slot, d], wide_r.at[slot, d],
                   "seq", lax.rem(at_seq + d, m))
            for d in range(1, m)
        ]
        for copy in copies:
            copy.start()
        for d, copy in enumerate(copies):
            copy.wait()
            value = value + wide[slot, d + 1]
        return value

    def settle(k, slot):
        scale_out[...] = by_token(feat_sum(0))

        def image_block(at, sums):
            cols = columns(at, lanes)
            image = held[:, cols] * scale_out[...] * gain_out[me, :, cols]
            residual = image - out[:, cols]
            images[k, :, cols] = image
            residuals[k, :, cols] = residual
            first = residuals[0, :, cols]
            pairs = [residual * residuals[j, :, cols] for j in range(ITERS)] + [first * first]
            return tuple(
                one + jnp.sum(pair.reshape(toks // 8, 8, lanes), axis=0) for one, pair in zip(sums, pairs)
            )

        zero = jnp.zeros((8, lanes), f32)
        sums = lax.fori_loop(0, blocks_of(part), image_block, (zero,) * (ITERS + 1))

        @pl.when(k > 0)
        def _():
            rows = [jnp.sum(one, axis=0, keepdims=True) for one in sums]
            mail_out[2] = jnp.concatenate(rows + [jnp.zeros((8 - len(rows), lanes), f32)], axis=0)
            total = seq_sum(slot, feat_sum(2))
            total = jnp.broadcast_to(jnp.sum(total, axis=1, keepdims=True), (8, lanes))
            values = [jnp.broadcast_to(total[j : j + 1], (8, lanes)) for j in range(ITERS + 1)]
            gram[0] = values[ITERS]
            for j in range(ITERS):
                gram[ITERS * k + j] = values[j]
                gram[ITERS * j + k] = values[j]
            system = []
            for i in range(ITERS):
                row = []
                for j in range(ITERS):
                    fixed = LAMBDA if i == j else 0.0
                    there = gram[ITERS * i + j] / scale_all + fixed
                    row.append(jnp.where(max(i, j) <= k, there, 1.0 if i == j else 0.0))
                system.append(row)
            goals = [jnp.where(i <= k, jnp.ones((8, lanes), f32), 0.0) for i in range(ITERS)]
            unscaled = solve_values(system, goals)
            whole = unscaled[0]
            for value in unscaled[1:]:
                whole = whole + value
            for j in range(ITERS):
                coef[j] = unscaled[j] / whole

        def mix_block(at, total):
            cols = columns(at, lanes)
            tiles = [jnp.broadcast_to(coef[j][:1], (toks, lanes)) for j in range(ITERS)]
            current = tiles[0] * images[0, :, cols]
            for j in range(1, ITERS):
                current = current + tiles[j] * images[j, :, cols]
            out[:, cols] = current
            mixed = current + inj[:, cols].astype(f32)
            return total + mixed * mixed

        mail_out[1] = row_sums(lax.fori_loop(0, blocks_of(part), mix_block, zero_tile))

    def kv_copy(slot, c, owner, sems, target):
        here = kv.at[slot, owner, pl.ds(c * half, half)]
        return remote(here, here, sems[0], sems[1], "seq", target)

    def up_step(slot, c, d, owner, target):
        return kv_copy(slot, c, owner, (up_s.at[c, d], up_r.at[slot, c, d]), target)

    def side_step(slot, c, k, owner):
        return kv_copy(slot, c, owner, (side_s.at[c, k], side_r.at[slot, c, k]), row_partner)

    def gathered(buffer):
        return jnp.concatenate([buffer[f] for f in range(n)], axis=1)

    def project(buffer, weights, cols):
        return jnp.dot(gathered(buffer), weights[:, cols], preferred_element_type=f32)

    def combined(cols, size):
        total = proj[ITERS - 1, :, cols]
        for j in range(ITERS - 1):
            total = total + jnp.broadcast_to(coef[j][:1, :1], (toks, size)) * proj[j, :, cols]
        return total

    def wide_scale(ref, size):
        return jnp.concatenate([ref[...]] * (size // lanes), axis=1)

    q_tile = span
    kv_tile = min(256, 2 * kv_cols)

    def attend(slot, k):
        owner = 2 * (level - k)
        which = jnp.minimum(k, 1)
        for e in range(kv_local):
            keys = kv[slot, pl.ds(owner, 2), :, e * HEAD_DIM : (e + 1) * HEAD_DIM].reshape(2 * toks, HEAD_DIM)
            values = kv[
                slot, pl.ds(owner, 2), :, kv_cols + e * HEAD_DIM : kv_cols + (e + 1) * HEAD_DIM
            ].reshape(2 * toks, HEAD_DIM)
            values = jnp.concatenate([values, jnp.ones((2 * toks, HEAD_DIM), bf16)], axis=1)
            asked = queries[e * group : (e + 1) * group].reshape(group * toks, HEAD_DIM)
            scores = lax.dot_general(asked, keys, (((1,), (1,)), ((), ())), preferred_element_type=f32)
            scores = (scores.reshape(group, toks, 2 * toks) + bias[which][None]).reshape(group * toks, 2 * toks)
            old = top[e]
            new = jnp.maximum(old, jnp.max(scores, axis=1, keepdims=True))
            top[e] = new
            both = jnp.concatenate([new] * (2 * toks // lanes), axis=1)
            weights = jnp.exp2((scores - both) * factor)
            fade = jnp.exp2((old - new) * factor)
            acc[e] = acc[e] * jnp.concatenate([fade, fade], axis=1) + jnp.dot(
                weights.astype(bf16), values, preferred_element_type=f32
            )

    def near_step(c, d):
        return remote(
            near_out.at[d, :, columns(c, span)], near.at[d, :, columns(c, span)],
            near_s.at[c, d], near_r.at[c, d], "feat", partner,
        )

    def far_step(c, d):
        return remote(
            outgoing.at[d, :, columns(c, span)], far.at[d, :, columns(c, span)],
            far_s.at[c, d], far_r.at[c, d], "feat", 2 * lined[d] + side,
        )

    def out_dot(target, c):
        cols = pl.ds(pl.multiple_of(target * part + c * span, span), span)
        return jnp.dot(attended[...], w_o[:, cols], preferred_element_type=f32)

    def pass_on(c):
        cols = columns(c, span)
        for d in range(1, lines):
            near_step(c, d).wait_recv()
            outgoing[d, :, cols] = (keep[d, :, cols] + near[d, :, cols].astype(f32)).astype(bf16)
            far_step(c, d).start()

    def own_dots(c):
        cols = columns(c, span)
        near_out[0, :, cols] = out_dot(2 * mine + 1 - side, c).astype(bf16)
        near_step(c, 0).start()
        keep[0, :, cols] = out_dot(me, c)

    def evaluate(it):
        slot = lax.rem(it, 2)
        k = jnp.maximum(it - 1, 0)
        scale_in[...] = by_token(feat_sum(1))

        @pl.when(it == 0)
        def _():
            loads[2].wait()
            loads[3].wait()

        @pl.when(it == 1)
        def _():
            for d in range(1, lines):
                inj_forward(d).wait()
            inj_step(0).wait()
            for d in range(1, lines):
                inj_step(d).wait_send()

            @pl.loop(0, 2 * kv_cols // kv_tile)
            def _(at):
                cols = columns(at, kv_tile)
                proj[ITERS - 1, :, cols] = project(tok_inj, w_kv, cols)

            @pl.loop(0, head_cols // q_tile)
            def _(at):
                put = pl.ds(pl.multiple_of(2 * kv_cols + at * q_tile, q_tile), q_tile)
                proj[ITERS - 1, :, put] = project(tok_inj, w_q, columns(at, q_tile))

        @pl.loop(0, CHUNKS)
        def _(c):
            for d in range(1, lines):
                gather_step(c, d).wait_recv()
                forward_step(c, d).start()

        @pl.loop(0, CHUNKS)
        def _(c):
            gather_step(c, 0).wait()
            for d in range(1, lines):
                forward_step(c, d).wait()
                gather_step(c, d).wait_send()

        @pl.loop(0, 2 * kv_cols // kv_tile)
        def _(at):
            cols = columns(at, kv_tile)
            proj[k, :, cols] = project(tok, w_kv, cols) * wide_scale(scale_out, kv_tile)
            kv[slot, at_seq, :, cols] = (combined(cols, kv_tile) * wide_scale(scale_in, kv_tile)).astype(bf16)

        for c in range(HALVES):
            @pl.when(row_side == 0)
            def _():
                side_step(slot, c, 0, at_seq).start()

            for d in range(levels - 1, 0, -1):
                @pl.when(level + d < levels)
                def _():
                    up_step(slot, c, d, at_seq, at_seq + 2 * d).start()

        @pl.when(it == 0)
        def _():
            loads[4].wait()

        @pl.loop(0, head_cols // q_tile)
        def _(at):
            put = pl.ds(pl.multiple_of(2 * kv_cols + at * q_tile, q_tile), q_tile)
            proj[k, :, put] = project(tok, w_q, columns(at, q_tile)) * wide_scale(scale_out, q_tile)
            asked = (combined(put, q_tile) * wide_scale(scale_in, q_tile)).astype(bf16)
            for h in range(q_tile // HEAD_DIM):
                queries[at * (q_tile // HEAD_DIM) + h] = asked[:, h * HEAD_DIM : (h + 1) * HEAD_DIM]

        for e in range(kv_local):
            top[e] = jnp.full(top.shape[1:], -1e30, f32)
            acc[e] = jnp.zeros(acc.shape[1:], f32)

        @pl.loop(0, level + 1)
        def _(k):
            @pl.when(k + 1 <= level)
            def _():
                owner = at_seq - 2 * (k + 1)
                for c in range(HALVES):
                    up_step(slot, c, k + 1, owner, owner).wait_recv()
                    side_step(slot, c, k + 1, owner).start()

            @pl.when(k + row_side > 0)
            def _():
                for c in range(HALVES):
                    side_step(slot, c, k, row_partner - 2 * k).wait_recv()

            attend(slot, k)

        for e in range(kv_local):
            for g in range(group):
                rows = slice(g * toks, (g + 1) * toks)
                at = (e * group + g) * HEAD_DIM
                attended[:, at : at + HEAD_DIM] = (
                    acc[e, rows, :HEAD_DIM] / acc[e, rows, HEAD_DIM:]
                ).astype(bf16)

        @pl.when(it == 0)
        def _():
            loads[5].wait()
            for d in range(1, lines):
                inj_step(d).wait_recv()
                inj_forward(d).start()

        @pl.loop(0, CHUNKS)
        def _(c):
            cols = columns(c, span)
            for d in range(1, lines):
                near_out[d, :, cols] = out_dot(2 * lined[d] + 1 - side, c).astype(bf16)
                near_step(c, d).start()
                keep[d, :, cols] = out_dot(2 * lined[d] + side, c)

            @pl.when(c > 0)
            def _():
                pass_on(c - 1)

        own_dots(0)
        pass_on(CHUNKS - 1)

        @pl.loop(1, CHUNKS)
        def _(c):
            own_dots(c)

        def finish(c, total):
            near_step(c, 0).wait()
            for d in range(1, lines):
                near_step(c, d).wait_send()
                far_step(c, d).wait()
            for at in range(span // lanes):
                cols = pl.ds(pl.multiple_of(c * span + at * lanes, lanes), lanes)
                update = keep[0, :, cols] + near[0, :, cols].astype(f32)
                for d in range(1, lines):
                    update = update + far[d, :, cols].astype(f32)
                summed = out[:, cols] + inj[:, cols].astype(f32) + update
                held[:, cols] = summed
                tok[me, :, cols] = (summed * gain_out[me, :, cols] * gain_in[me, :, cols]).astype(bf16)
                total = total + summed * summed

            @pl.when(it + 1 < ITERS)
            def _():
                for d in range(1, lines):
                    gather_step(c, d).start()
                gather_step(c, 0).start()

            return total

        mail_out[0] = row_sums(lax.fori_loop(0, CHUNKS, finish, zero_tile))

        for c in range(HALVES):
            @pl.when(row_side == 0)
            def _():
                side_step(slot, c, 0, at_seq).wait_send()

            for d in range(levels - 1, 0, -1):
                @pl.when(level + d < levels)
                def _():
                    up_step(slot, c, d, at_seq, at_seq + 2 * d).wait_send()

        @pl.loop(1, level + 1)
        def _(k):
            for c in range(HALVES):
                side_step(slot, c, k, at_seq - 2 * k).wait_send()

    @pl.loop(0, ITERS + 1)
    def _(it):
        @pl.when(it > 0)
        def _():
            settle(it - 1, lax.rem(it, 2))

        @pl.when(it < ITERS)
        def _():
            evaluate(it)


def on_device(injection, warm_start, gain_in, gain_out, w_query, w_key, w_value, w_out):
    n, m = lax.axis_size("feat"), lax.axis_size("seq")
    toks, part = injection.shape
    head_cols, kv_cols = w_query.shape[1], w_key.shape[1]
    kv_local = kv_cols // HEAD_DIM
    group = HEADS // KV_HEADS
    lines = n // 2
    f32, bf16 = jnp.float32, jnp.bfloat16
    vmem, dma = pltpu.VMEM, pltpu.SemaphoreType.DMA
    lanes = 128
    scratch = [
        vmem((n, toks, part), bf16), vmem((n, toks, part), bf16),
        vmem((w_key.shape[0], 2 * kv_cols), bf16), vmem(w_query.shape, bf16), vmem(w_out.shape, bf16),
        vmem((toks, part), bf16), vmem((toks, part), bf16),
        vmem((ITERS, toks, part), f32), vmem((ITERS, toks, part), f32), vmem((toks, part), f32),
        vmem((ITERS, toks, head_cols + 2 * kv_cols), f32),
        vmem((head_cols // HEAD_DIM, toks, HEAD_DIM), bf16),
        vmem((2, m, toks, 2 * kv_cols), bf16),
        vmem((kv_local, group * toks, 2 * HEAD_DIM), f32), vmem((kv_local, group * toks, lanes), f32),
        vmem((2, toks, 2 * toks), f32), vmem((toks, head_cols), bf16),
        vmem((lines, toks, part), f32),
        vmem((lines, toks, part), bf16), vmem((lines, toks, part), bf16),
        vmem((lines, toks, part), bf16), vmem((lines, toks, part), bf16),
        vmem((ITERS, 8, lanes), f32), vmem((ITERS * ITERS, 8, lanes), f32),
        vmem((toks, lanes), f32), vmem((toks, lanes), f32),
        vmem((3, 8, toks), f32), vmem((3, n, 8, toks), f32),
        vmem((8, lanes), f32), vmem((2, m, 8, lanes), f32),
        dma((6,)), dma((CHUNKS, n)), dma((CHUNKS, n)), dma((n,)), dma((n,)),
        dma((HALVES, m // 2)), dma((2, HALVES, m // 2)), dma((HALVES, m // 2)), dma((2, HALVES, m // 2)),
        dma((CHUNKS, lines)), dma((CHUNKS, lines)), dma((CHUNKS, lines)), dma((CHUNKS, lines)),
        dma((3, n)), dma((3, n)), dma((2, m)), dma((2, m)),
    ]
    return pl.pallas_call(
        functools.partial(whole_kernel, n, m),
        out_shape=jax.ShapeDtypeStruct((toks, part), f32),
        in_specs=[ANY, ANY, VMEM, VMEM, ANY, ANY, ANY, ANY],
        out_specs=VMEM,
        scratch_shapes=scratch,
        compiler_params=pltpu.CompilerParams(
            collective_id=0, has_side_effects=True, vmem_limit_bytes=63 * 1024 * 1024
        ),
    )(
        injection, warm_start, gain_in.reshape(n, 1, part), gain_out.reshape(n, 1, part),
        w_query, w_key, w_value, w_out,
    )


def solution(mesh):
    in_specs = (
        P("seq", "feat"),
        P("seq", "feat"),
        P(),
        P(),
        P(None, "feat"),
        P(None, "feat"),
        P(None, "feat"),
        P("feat", None),
    )
    out_specs = P("seq", "feat")
    return jax.shard_map(
        on_device, mesh=mesh, in_specs=in_specs, out_specs=out_specs, check_vma=False
    )
```

profile of v0, /device:TPU:0, one launch (start us, length us, event | category | flops | bytes accessed | tf_op | source)
XLA Modules:
  0.0 212.3 jit_solution(11349584313413778259)
XLA Ops:
  0.0 210.4 %shard_map.82 = f32[128,1280]{1,0:T(8,128)} custom-call(bf16[128,1280]{1,0:T(8,128)(2,1)} %inj_hbm.1, bf16[128,1280]{1,0:T(8,128)(2,1)} %warm_hbm.1, f32[4,1,1280]{2,1,0:T(1,128)} %bitcast.2, f32[4,1,1280]{2,1,0:T(1,128)} %bitcast.3, bf16[5120,1280]{1,0:T(8,128)(2,1)} %wq_hbm.1, bf16[5120,256]{1,0:T(8,128)(2,1)} %wk_hbm.1, bf16[5120,256]{1,0:T(8,128)(2,1)} %wv_hbm.1, ...), custom_call_target="tpu_custom_call" | custom-call | tf_op jit(solution)/shard_map/pallas_call | solution.py:562
  210.4 2.0 copy.10
where the time goes:
time: 213 us; the launch traced here: 212 us
  Pallas kernels  210 us (99%)
    pallas_call x1, Pallas kernels, on_device(): pl.pallas_call(functools.partial(whole_kernel, n, m), out_shape=jax.Shape...  210 us

commit v1 on v0

--- a/solution.py
+++ b/solution.py
@@ -16,7 +16,11 @@
 EPS = 1e-06
 LAMBDA = 0.03
 CHUNKS = 5
-HALVES = 2
+HALVES = 4
+EARLY = 3
+ROWS = 7
+WARM = ITERS
+INJ = ITERS + 1
 MESH = pl.DeviceIdType.MESH
 VMEM = pl.BlockSpec(memory_space=pltpu.VMEM)
 ANY = pl.BlockSpec(memory_space=pl.ANY)
@@ -49,8 +53,8 @@
 
 
 def whole_kernel(n, m, inj_hbm, warm_hbm, gain_in, gain_out, wq_hbm, wk_hbm, wv_hbm, wo_hbm, out,
-                 tok, tok_inj, w_kv, w_q, w_o, inj, warm, images, residuals, held, proj, queries, kv,
-                 acc, top, bias, attended, keep, near_out, near, outgoing, far, coef, gram,
+                 tok, tok_inj, w_kv, w_q, w_o, inj, warm, images, held, proj, queries, kv,
+                 acc, top, bias, attended, keep, near_out, near, outgoing, far, coef, gram, dots, totals, mixing, sums,
                  scale_out, scale_in, mail_out, mail, wide_out, wide,
                  load_sem, feat_s, feat_r, inj_s, inj_r, up_s, up_r, side_s, side_r,
                  near_s, near_r, far_s, far_r, mail_s, mail_r, wide_s, wide_r):
@@ -104,12 +108,18 @@
     def blocks_of(ref_width):
         return ref_width // lanes
 
-    def row_sums(partial):
-        return jnp.broadcast_to(jnp.sum(partial.T, axis=0, keepdims=True), (8, toks))
-
-    def by_token(total):
-        scale = lax.rsqrt(total * (1.0 / width) + EPS)
-        return jnp.broadcast_to(scale[:1], (lanes, toks)).T
+    def row_sums(partials):
+        rows = [jnp.sum(partial.T, axis=0, keepdims=True) for partial in partials]
+        return jnp.concatenate(rows + [jnp.zeros((8 - len(rows), toks), f32)], axis=0)
+
+    def inverse_rms(total):
+        return lax.rsqrt(total * (1.0 / width) + EPS)
+
+    def by_token(row):
+        return jnp.broadcast_to(row[:1], (lanes, toks)).T
+
+    def everywhere(row):
+        return jnp.broadcast_to(row, (8, row.shape[1]))
 
     zero_tile = jnp.zeros((toks, lanes), f32)
 
@@ -118,7 +128,6 @@
         cols = columns(at, lanes)
         for j in range(ITERS):
             images[j, :, cols] = zero_tile
-            residuals[j, :, cols] = zero_tile
 
     @pl.loop(0, blocks_of(head_cols + 2 * kv_cols))
     def _(at):
@@ -126,10 +135,17 @@
         for j in range(ITERS):
             proj[j, :, cols] = zero_tile
 
+    small_zero = jnp.zeros((8, lanes), f32)
     for j in range(ITERS):
         coef[j] = jnp.full((8, lanes), 1.0 if j == 0 else 0.0, f32)
     for j in range(ITERS * ITERS):
-        gram[j] = jnp.zeros((8, lanes), f32)
+        gram[j] = small_zero
+    for j in range((WARM + 1) * (WARM + 1)):
+        totals[j] = small_zero
+    for j in range(ITERS * (WARM + 1)):
+        mixing[j] = small_zero
+    for j in range((INJ + 1) * (INJ + 1)):
+        dots[j] = jnp.zeros((8, toks), f32)
     scale_out[...] = jnp.ones((toks, lanes), f32)
 
     @pl.when(row_side == 0)
@@ -168,7 +184,7 @@
         at = lines - 1 + d
         return forward_copy(tok_inj, pl.ds(0, part), (inj_s.at[at], inj_r.at[at]), d)
 
-    def start_block(at, total):
+    def start_block(at, totals_now):
         cols = columns(at, lanes)
         gain = gain_in[me, :, cols]
         base = inj[:, cols].astype(f32)
@@ -177,75 +193,116 @@
         mixed = first + base
         tok[me, :, cols] = (mixed * gain).astype(bf16)
         tok_inj[me, :, cols] = (base * gain).astype(bf16)
-        return total + mixed * mixed
-
-    total = lax.fori_loop(0, blocks_of(part), start_block, zero_tile)
-    mail_out[1] = row_sums(total)
-    pl.semaphore_wait(barrier, n + m - 2)
-    for c in range(CHUNKS):
-        for d in range(1, lines):
-            gather_step(c, d).start()
-        gather_step(c, 0).start()
-    for d in range(lines):
-        inj_step(d).start()
-
-    def feat_sum(which):
-        copies = [
+        pairs = (first * first, base * base, mixed * mixed)
+        return tuple(total + pair for total, pair in zip(totals_now, pairs))
+
+    mail_out[1] = row_sums(lax.fori_loop(0, blocks_of(part), start_block, (zero_tile,) * 3))
+
+    def mail_copies(which):
+        return [
             remote(mail_out.at[which], mail.at[which, d], mail_s.at[which, d], mail_r.at[which, d],
                    "feat", lax.rem(me + d, n))
             for d in range(1, n)
         ]
-        for copy in copies:
+
+    def mail_start(which):
+        for copy in mail_copies(which):
             copy.start()
+
+    def mail_total(which):
         total = mail_out[which]
-        for d, copy in enumerate(copies):
+        for d, copy in enumerate(mail_copies(which)):
             copy.wait()
             total = total + mail[which, d + 1]
         return total
 
-    def seq_sum(slot, value):
-        wide_out[...] = value
-        copies = [
+    def wide_copies(slot):
+        return [
             remote(wide_out, wide.at[slot, d], wide_s.at[slot, d], wide_r.at[slot, d],
                    "seq", lax.rem(at_seq + d, m))
             for d in range(1, m)
         ]
-        for copy in copies:
-            copy.start()
-        for d, copy in enumerate(copies):
+
+    def wide_total(slot):
+        total = wide_out[...]
+        for d, copy in enumerate(wide_copies(slot)):
             copy.wait()
-            value = value + wide[slot, d + 1]
-        return value
-
-    def settle(k, slot):
-        scale_out[...] = by_token(feat_sum(0))
-
-        def image_block(at, sums):
-            cols = columns(at, lanes)
-            image = held[:, cols] * scale_out[...] * gain_out[me, :, cols]
-            residual = image - out[:, cols]
-            images[k, :, cols] = image
-            residuals[k, :, cols] = residual
-            first = residuals[0, :, cols]
-            pairs = [residual * residuals[j, :, cols] for j in range(ITERS)] + [first * first]
-            return tuple(
-                one + jnp.sum(pair.reshape(toks // 8, 8, lanes), axis=0) for one, pair in zip(sums, pairs)
-            )
-
-        zero = jnp.zeros((8, lanes), f32)
-        sums = lax.fori_loop(0, blocks_of(part), image_block, (zero,) * (ITERS + 1))
+            total = total + wide[slot, d + 1]
+        return total
+
+    def start_gather(c):
+        for d in range(1, lines):
+            gather_step(c, d).start()
+        gather_step(c, 0).start()
+
+    def relay(c):
+        for d in range(1, lines):
+            gather_step(c, d).wait_recv()
+            forward_step(c, d).start()
+
+    pl.semaphore_wait(barrier, n + m - 2)
+    mail_start(1)
+    for c in range(CHUNKS):
+        start_gather(c)
+
+    def dot_at(i, j):
+        return dots[(INJ + 1) * i + j]
+
+    def total_at(i, j):
+        return totals[(WARM + 1) * i + j]
+
+    def settle(k, slot, more):
+        total = mail_total(0)
+        rate = inverse_rms(total[:1])
+        scale_out[...] = by_token(rate)
+        for at, j in enumerate(list(range(ITERS - 1)) + [WARM, INJ]):
+            value = everywhere(total[at + 1 : at + 2] * rate)
+            dots[(INJ + 1) * k + j] = value
+            dots[(INJ + 1) * j + k] = value
+        dots[(INJ + 2) * k] = everywhere(total[ROWS - 1 : ROWS] * rate * rate)
+        for j in range(WARM + 1):
+            before_now = jnp.where(k == 0, 1.0 if j == WARM else 0.0, coef[j] if j < WARM else 0.0)
+            mixing[(WARM + 1) * k + j] = jnp.where(k == j, 1.0, 0.0) - before_now * jnp.ones((8, lanes), f32)
 
         @pl.when(k > 0)
         def _():
-            rows = [jnp.sum(one, axis=0, keepdims=True) for one in sums]
-            mail_out[2] = jnp.concatenate(rows + [jnp.zeros((8 - len(rows), lanes), f32)], axis=0)
-            total = seq_sum(slot, feat_sum(2))
-            total = jnp.broadcast_to(jnp.sum(total, axis=1, keepdims=True), (8, lanes))
-            values = [jnp.broadcast_to(total[j : j + 1], (8, lanes)) for j in range(ITERS + 1)]
-            gram[0] = values[ITERS]
+            rows = [dots[(INJ + 1) * k + j][:1] for j in range(WARM + 1)]
+            rows = rows + [dot_at(0, 0)[:1], dot_at(0, WARM)[:1], dot_at(WARM, WARM)[:1]]
+            wide_out[...] = jnp.concatenate(rows, axis=0)
+            for copy in wide_copies(slot):
+                copy.start()
+
+        @pl.when(more)
+        def _():
+            for c in range(EARLY):
+                relay(c)
+
+        @pl.when(k > 0)
+        def _():
+            total = jnp.broadcast_to(jnp.sum(wide_total(slot), axis=1, keepdims=True), (8, lanes))
+            values = [jnp.broadcast_to(total[j : j + 1], (8, lanes)) for j in range(8)]
+            for j in range(WARM + 1):
+                totals[(WARM + 1) * k + j] = values[j]
+                totals[(WARM + 1) * j + k] = values[j]
+            totals[0] = values[WARM + 1]
+            totals[WARM] = values[WARM + 2]
+            totals[(WARM + 1) * WARM] = values[WARM + 2]
+            totals[(WARM + 1) * WARM + WARM] = values[WARM + 3]
+
+            def product(i, j):
+                run = small_zero
+                for a in range(WARM + 1):
+                    inner = small_zero
+                    for b in range(WARM + 1):
+                        inner = inner + total_at(a, b) * mixing[(WARM + 1) * j + b]
+                    run = run + mixing[(WARM + 1) * i + a] * inner
+                return run
+
+            gram[0] = product(0, 0)
             for j in range(ITERS):
-                gram[ITERS * k + j] = values[j]
-                gram[ITERS * j + k] = values[j]
+                value = product(j, k)
+                gram[ITERS * k + j] = value
+                gram[ITERS * j + k] = value
             system = []
             for i in range(ITERS):
                 row = []
@@ -262,24 +319,31 @@
             for j in range(ITERS):
                 coef[j] = unscaled[j] / whole
 
-        def mix_block(at, total):
+        parts_now = [jnp.broadcast_to(coef[j][:, :1], (8, toks)) for j in range(ITERS)]
+        square = dot_at(INJ, INJ)
+        for i in range(ITERS):
+            inner = 2.0 * dot_at(i, INJ)
+            for j in range(ITERS):
+                inner = inner + parts_now[j] * dot_at(i, j)
+            square = square + parts_now[i] * inner
+        scale_in[...] = by_token(inverse_rms(jnp.maximum(square, 0.0)))
+
+    def remix(k):
+        @pl.loop(0, blocks_of(part))
+        def _(at):
             cols = columns(at, lanes)
-            tiles = [jnp.broadcast_to(coef[j][:1], (toks, lanes)) for j in range(ITERS)]
-            current = tiles[0] * images[0, :, cols]
+            images[k, :, cols] = held[:, cols] * scale_out[...] * gain_out[me, :, cols]
+            current = coef[0][:1] * images[0, :, cols]
             for j in range(1, ITERS):
-                current = current + tiles[j] * images[j, :, cols]
+                current = current + coef[j][:1] * images[j, :, cols]
             out[:, cols] = current
-            mixed = current + inj[:, cols].astype(f32)
-            return total + mixed * mixed
-
-        mail_out[1] = row_sums(lax.fori_loop(0, blocks_of(part), mix_block, zero_tile))
 
     def kv_copy(slot, c, owner, sems, target):
         here = kv.at[slot, owner, pl.ds(c * half, half)]
         return remote(here, here, sems[0], sems[1], "seq", target)
 
-    def up_step(slot, c, d, owner, target):
-        return kv_copy(slot, c, owner, (up_s.at[c, d], up_r.at[slot, c, d]), target)
+    def up_step(slot, c, k, owner, target):
+        return kv_copy(slot, c, owner, (up_s.at[c, k], up_r.at[slot, c, k]), target)
 
     def side_step(slot, c, k, owner):
         return kv_copy(slot, c, owner, (side_s.at[c, k], side_r.at[slot, c, k]), row_partner)
@@ -353,13 +417,29 @@
         near_step(c, 0).start()
         keep[0, :, cols] = out_dot(me, c)
 
-    def evaluate(it):
+    def arrive(slot, k):
+        @pl.when(k <= level)
+        def _():
+            owner = at_seq - 2 * k
+            for c in range(HALVES):
+                up_step(slot, c, k - 1, owner, owner).wait_recv()
+
+                @pl.when(level + 1 < levels)
+                def _():
+                    up_step(slot, c, k, owner, at_seq + 2).start()
+
+                side_step(slot, c, k, owner).start()
+
+    def send_keys(it):
         slot = lax.rem(it, 2)
         k = jnp.maximum(it - 1, 0)
-        scale_in[...] = by_token(feat_sum(1))
 
         @pl.when(it == 0)
         def _():
+            total = mail_total(1)
+            dots[(INJ + 1) * WARM + WARM] = everywhere(total[:1])
+            dots[(INJ + 1) * INJ + INJ] = everywhere(total[1:2])
+            scale_in[...] = by_token(inverse_rms(total[2:3]))
             loads[2].wait()
             loads[3].wait()
 
@@ -381,11 +461,9 @@
                 put = pl.ds(pl.multiple_of(2 * kv_cols + at * q_tile, q_tile), q_tile)
                 proj[ITERS - 1, :, put] = project(tok_inj, w_q, columns(at, q_tile))
 
-        @pl.loop(0, CHUNKS)
+        @pl.loop(jnp.where(it > 0, EARLY, 0), CHUNKS)
         def _(c):
-            for d in range(1, lines):
-                gather_step(c, d).wait_recv()
-                forward_step(c, d).start()
+            relay(c)
 
         @pl.loop(0, CHUNKS)
         def _(c):
@@ -405,14 +483,15 @@
             def _():
                 side_step(slot, c, 0, at_seq).start()
 
-            for d in range(levels - 1, 0, -1):
-                @pl.when(level + d < levels)
-                def _():
-                    up_step(slot, c, d, at_seq, at_seq + 2 * d).start()
+            @pl.when(level + 1 < levels)
+            def _():
+                up_step(slot, c, 0, at_seq, at_seq + 2).start()
 
         @pl.when(it == 0)
         def _():
             loads[4].wait()
+            for d in range(lines):
+                inj_step(d).start()
 
         @pl.loop(0, head_cols // q_tile)
         def _(at):
@@ -426,14 +505,16 @@
             top[e] = jnp.full(top.shape[1:], -1e30, f32)
             acc[e] = jnp.zeros(acc.shape[1:], f32)
 
+        arrive(slot, 1)
+
+    def finish_layer(it):
+        slot = lax.rem(it, 2)
+
         @pl.loop(0, level + 1)
         def _(k):
-            @pl.when(k + 1 <= level)
-            def _():
-                owner = at_seq - 2 * (k + 1)
-                for c in range(HALVES):
-                    up_step(slot, c, k + 1, owner, owner).wait_recv()
-                    side_step(slot, c, k + 1, owner).start()
+            @pl.when(k > 0)
+            def _():
+                arrive(slot, k + 1)
 
             @pl.when(k + row_side > 0)
             def _():
@@ -476,7 +557,11 @@
         def _(c):
             own_dots(c)
 
-        def finish(c, total):
+        for at in range(ROWS):
+            sums[at] = zero_tile
+
+        @pl.loop(0, CHUNKS)
+        def _(c):
             near_step(c, 0).wait()
             for d in range(1, lines):
                 near_step(c, d).wait_send()
@@ -486,45 +571,64 @@
                 update = keep[0, :, cols] + near[0, :, cols].astype(f32)
                 for d in range(1, lines):
                     update = update + far[d, :, cols].astype(f32)
-                summed = out[:, cols] + inj[:, cols].astype(f32) + update
+                base = inj[:, cols].astype(f32)
+                summed = out[:, cols] + base + update
                 held[:, cols] = summed
-                tok[me, :, cols] = (summed * gain_out[me, :, cols] * gain_in[me, :, cols]).astype(bf16)
-                total = total + summed * summed
-
-            @pl.when(it + 1 < ITERS)
-            def _():
-                for d in range(1, lines):
-                    gather_step(c, d).start()
-                gather_step(c, 0).start()
-
-            return total
-
-        mail_out[0] = row_sums(lax.fori_loop(0, CHUNKS, finish, zero_tile))
+                scaled = summed * gain_out[me, :, cols]
+                tok[me, :, cols] = (scaled * gain_in[me, :, cols]).astype(bf16)
+                others = [images[j, :, cols] for j in range(ITERS - 1)]
+                others = others + [warm[:, cols].astype(f32), base, scaled]
+                sums[0] += summed * summed
+                for row, other in enumerate(others):
+                    sums[row + 1] += scaled * other
+
+            @pl.when((it + 1 < ITERS) & (c == CHUNKS - 2))
+            def _():
+                start_gather(0)
+
+        mail_out[0] = row_sums([sums[at] for at in range(ROWS)])
+        mail_start(0)
+
+        @pl.when(it + 1 < ITERS)
+        def _():
+            for c in range(1, CHUNKS):
+                start_gather(c)
 
         for c in range(HALVES):
             @pl.when(row_side == 0)
             def _():
                 side_step(slot, c, 0, at_seq).wait_send()
 
-            for d in range(levels - 1, 0, -1):
-                @pl.when(level + d < levels)
-                def _():
-                    up_step(slot, c, d, at_seq, at_seq + 2 * d).wait_send()
+            @pl.when(level + 1 < levels)
+            def _():
+                up_step(slot, c, 0, at_seq, at_seq + 2).wait_send()
 
         @pl.loop(1, level + 1)
         def _(k):
             for c in range(HALVES):
                 side_step(slot, c, k, at_seq - 2 * k).wait_send()
 
+                @pl.when(level + 1 < levels)
+                def _():
+                    up_step(slot, c, k, at_seq - 2 * k, at_seq + 2).wait_send()
+
     @pl.loop(0, ITERS + 1)
     def _(it):
         @pl.when(it > 0)
         def _():
-            settle(it - 1, lax.rem(it, 2))
+            settle(it - 1, lax.rem(it, 2), it < ITERS)
 
         @pl.when(it < ITERS)
         def _():
-            evaluate(it)
+            send_keys(it)
+
+        @pl.when(it > 0)
+        def _():
+            remix(it - 1)
+
+        @pl.when(it < ITERS)
+        def _():
+            finish_layer(it)
 
 
 def on_device(injection, warm_start, gain_in, gain_out, w_query, w_key, w_value, w_out):
@@ -541,7 +645,7 @@
         vmem((n, toks, part), bf16), vmem((n, toks, part), bf16),
         vmem((w_key.shape[0], 2 * kv_cols), bf16), vmem(w_query.shape, bf16), vmem(w_out.shape, bf16),
         vmem((toks, part), bf16), vmem((toks, part), bf16),
-        vmem((ITERS, toks, part), f32), vmem((ITERS, toks, part), f32), vmem((toks, part), f32),
+        vmem((ITERS, toks, part), f32), vmem((toks, part), f32),
         vmem((ITERS, toks, head_cols + 2 * kv_cols), f32),
         vmem((head_cols // HEAD_DIM, toks, HEAD_DIM), bf16),
         vmem((2, m, toks, 2 * kv_cols), bf16),
@@ -551,6 +655,8 @@
         vmem((lines, toks, part), bf16), vmem((lines, toks, part), bf16),
         vmem((lines, toks, part), bf16), vmem((lines, toks, part), bf16),
         vmem((ITERS, 8, lanes), f32), vmem((ITERS * ITERS, 8, lanes), f32),
+        vmem(((INJ + 1) * (INJ + 1), 8, toks), f32), vmem(((WARM + 1) * (WARM + 1), 8, lanes), f32),
+        vmem((ITERS * (WARM + 1), 8, lanes), f32), vmem((ROWS, toks, lanes), f32),
         vmem((toks, lanes), f32), vmem((toks, lanes), f32),
         vmem((3, 8, toks), f32), vmem((3, n, 8, toks), f32),
         vmem((8, lanes), f32), vmem((2, m, 8, lanes), f32),

time: 213 us -> 163 us (0.77)
  Pallas kernels: 210 us -> 161 us
    pallas_call x1, Pallas kernels: 210 us -> 161 us  [on_device(): pl.pallas_call(functools.partial(whole_kernel, n, m), out_shape=jax.Shape...]
where the time goes in v1:
time: 163 us
  Pallas kernels  161 us (99%)
  local copies, waits for them, and re-layouts  1.97 us (1%)
    pallas_call x1, Pallas kernels, on_device(): pl.pallas_call(functools.partial(whole_kernel, n, m), out_shape=jax.Shape...  161 us

profile of v1, /device:TPU:0, one launch (start us, length us, event | category | flops | bytes accessed | tf_op | source)
XLA Modules:
  0.0 163.0 jit_solution(3527957512627483716)
XLA Ops:
  0.0 161.1 %shard_map.82 = f32[128,1280]{1,0:T(8,128)} custom-call(bf16[128,1280]{1,0:T(8,128)(2,1)} %inj_hbm.1, bf16[128,1280]{1,0:T(8,128)(2,1)} %warm_hbm.1, f32[4,1,1280]{2,1,0:T(1,128)} %bitcast.2, f32[4,1,1280]{2,1,0:T(1,128)} %bitcast.3, bf16[5120,1280]{1,0:T(8,128)(2,1)} %wq_hbm.1, bf16[5120,256]{1,0:T(8,128)(2,1)} %wk_hbm.1, bf16[5120,256]{1,0:T(8,128)(2,1)} %wv_hbm.1, ...), custom_call_target="tpu_custom_call" | custom-call | tf_op jit(solution)/shard_map/pallas_call | solution.py:668
  161.1 2.0 %copy.10 = f32[128,1280]{1,0:T(8,128)} copy(f32[128,1280]{1,0:T(8,128)} %shard_map.82) | data formatting | bytes 1310720

commit v2 on v1

--- a/solution.py
+++ b/solution.py
@@ -17,7 +17,6 @@
 LAMBDA = 0.03
 CHUNKS = 5
 HALVES = 4
-EARLY = 3
 ROWS = 7
 WARM = ITERS
 INJ = ITERS + 1
@@ -53,11 +52,11 @@
 
 
 def whole_kernel(n, m, inj_hbm, warm_hbm, gain_in, gain_out, wq_hbm, wk_hbm, wv_hbm, wo_hbm, out,
-                 tok, tok_inj, w_kv, w_q, w_o, inj, warm, images, held, proj, queries, kv,
-                 acc, top, bias, attended, keep, near_out, near, outgoing, far, coef, gram, dots, totals, mixing, sums,
+                 tok, tok_inj, w_kv, w_q, w_o, inj, warm, images, held, proj, base_proj, queries, kv,
+                 acc, top, bias, attended, keep, near_out, near, outgoing, far, coef, shares, gram, dots, totals, mixing, sums, norms_out, norms, blend,
                  scale_out, scale_in, mail_out, mail, wide_out, wide,
                  load_sem, feat_s, feat_r, inj_s, inj_r, up_s, up_r, side_s, side_r,
-                 near_s, near_r, far_s, far_r, mail_s, mail_r, wide_s, wide_r):
+                 near_s, near_r, far_s, far_r, mail_s, mail_r, wide_s, wide_r, norm_s, norm_r):
     me = lax.axis_index("feat")
     side = lax.rem(me, 2)
     mine = lax.div(me, 2)
@@ -96,6 +95,16 @@
     for load in loads:
         load.start()
 
+    f32_tile = jnp.zeros((8, toks), f32)
+    for slot in range(ITERS):
+        for owner in range(m):
+            norms[slot, owner] = f32_tile
+
+    @pl.when(row_side == 0)
+    def _():
+        for slot in range(ITERS):
+            kv[slot, at_seq + 1] = jnp.zeros(kv.shape[2:], bf16)
+
     barrier = pltpu.get_barrier_semaphore()
     for d in range(1, n):
         pl.semaphore_signal(barrier, inc=1, device_id={"feat": lax.rem(me + d, n)}, device_id_type=MESH)
@@ -123,66 +132,41 @@
 
     zero_tile = jnp.zeros((toks, lanes), f32)
 
-    @pl.loop(0, blocks_of(part))
-    def _(at):
-        cols = columns(at, lanes)
-        for j in range(ITERS):
-            images[j, :, cols] = zero_tile
-
-    @pl.loop(0, blocks_of(head_cols + 2 * kv_cols))
-    def _(at):
-        cols = columns(at, lanes)
-        for j in range(ITERS):
-            proj[j, :, cols] = zero_tile
-
-    small_zero = jnp.zeros((8, lanes), f32)
-    for j in range(ITERS):
-        coef[j] = jnp.full((8, lanes), 1.0 if j == 0 else 0.0, f32)
-    for j in range(ITERS * ITERS):
-        gram[j] = small_zero
-    for j in range((WARM + 1) * (WARM + 1)):
-        totals[j] = small_zero
-    for j in range(ITERS * (WARM + 1)):
-        mixing[j] = small_zero
-    for j in range((INJ + 1) * (INJ + 1)):
-        dots[j] = jnp.zeros((8, toks), f32)
-    scale_out[...] = jnp.ones((toks, lanes), f32)
-
-    @pl.when(row_side == 0)
-    def _():
-        for slot in range(2):
-            kv[slot, at_seq + 1] = jnp.zeros(kv.shape[2:], bf16)
-
-    key_at = lax.broadcasted_iota(jnp.int32, (toks, 2 * toks), 1)
-    query_at = lax.broadcasted_iota(jnp.int32, (toks, 2 * toks), 0) + row_side * toks
-    bias[0] = jnp.where(key_at <= query_at, 0.0, -1e30).astype(f32)
-    bias[1] = jnp.zeros((toks, 2 * toks), f32)
-
     loads[0].wait()
     loads[1].wait()
 
-    def gather_copy(buffer, cols, sems, d):
-        here = buffer.at[me, :, cols]
+    early = (CHUNKS - 1) * span
+    count = HALVES + 1
+
+    def gather_copy(buffer, rows, cols, sems, d):
+        here = buffer.at[me, rows, cols]
         target = partner if d == 0 else 2 * lined[d] + side
         return remote(here, here, sems[0], sems[1], "feat", target)
 
-    def forward_copy(buffer, cols, sems, d):
-        here = buffer.at[2 * before[d] + side, :, cols]
+    def forward_copy(buffer, rows, cols, sems, d):
+        here = buffer.at[2 * before[d] + side, rows, cols]
         return remote(here, here, sems[0], sems[1], "feat", partner)
 
-    def gather_step(c, d):
-        return gather_copy(tok, columns(c, span), (feat_s.at[c, d], feat_r.at[c, d]), d)
-
-    def forward_step(c, d):
+    def spot(p):
+        if isinstance(p, int) and p < 2:
+            return pl.ds(0, half), (pl.ds(0, early) if p == 0 else pl.ds(early, part - early))
+        return pl.ds(pl.multiple_of((p - 1) * half, half), half), pl.ds(0, part)
+
+    def gather_step(p, d):
+        return gather_copy(tok, *spot(p), (feat_s.at[p, d], feat_r.at[p, d]), d)
+
+    def forward_step(p, d):
         at = lines - 1 + d
-        return forward_copy(tok, columns(c, span), (feat_s.at[c, at], feat_r.at[c, at]), d)
+        return forward_copy(tok, *spot(p), (feat_s.at[p, at], feat_r.at[p, at]), d)
+
+    whole_spot = pl.ds(0, toks), pl.ds(0, part)
 
     def inj_step(d):
-        return gather_copy(tok_inj, pl.ds(0, part), (inj_s.at[d], inj_r.at[d]), d)
+        return gather_copy(tok_inj, *whole_spot, (inj_s.at[d], inj_r.at[d]), d)
 
     def inj_forward(d):
         at = lines - 1 + d
-        return forward_copy(tok_inj, pl.ds(0, part), (inj_s.at[at], inj_r.at[at]), d)
+        return forward_copy(tok_inj, *whole_spot, (inj_s.at[at], inj_r.at[at]), d)
 
     def start_block(at, totals_now):
         cols = columns(at, lanes)
@@ -196,6 +180,7 @@
         pairs = (first * first, base * base, mixed * mixed)
         return tuple(total + pair for total, pair in zip(totals_now, pairs))
 
+    zero_tile = jnp.zeros((toks, lanes), f32)
     mail_out[1] = row_sums(lax.fori_loop(0, blocks_of(part), start_block, (zero_tile,) * 3))
 
     def mail_copies(which):
@@ -230,20 +215,55 @@
             total = total + wide[slot, d + 1]
         return total
 
-    def start_gather(c):
+    def start_gather(p):
         for d in range(1, lines):
-            gather_step(c, d).start()
-        gather_step(c, 0).start()
-
-    def relay(c):
+            gather_step(p, d).start()
+        gather_step(p, 0).start()
+
+    def relay(p):
         for d in range(1, lines):
-            gather_step(c, d).wait_recv()
-            forward_step(c, d).start()
+            gather_step(p, d).wait_recv()
+            forward_step(p, d).start()
 
     pl.semaphore_wait(barrier, n + m - 2)
     mail_start(1)
-    for c in range(CHUNKS):
-        start_gather(c)
+    for p in range(count):
+        start_gather(p)
+
+    @pl.loop(0, blocks_of(part))
+    def _(at):
+        cols = columns(at, lanes)
+        for j in range(ITERS):
+            images[j, :, cols] = zero_tile
+
+    @pl.loop(0, blocks_of(head_cols))
+    def _(at):
+        cols = columns(at, lanes)
+        for j in range(ITERS):
+            proj[j, :, cols] = zero_tile
+
+    @pl.loop(0, blocks_of(head_cols + 2 * kv_cols))
+    def _(at):
+        base_proj[:, columns(at, lanes)] = zero_tile
+
+    small_zero = jnp.zeros((8, lanes), f32)
+    for j in range(ITERS):
+        coef[j] = jnp.full((8, lanes), 1.0 if j == 0 else 0.0, f32)
+        shares[j] = jnp.full((8, lanes), 1.0 if j == 0 else 0.0, f32)
+    for j in range(ITERS * ITERS):
+        gram[j] = small_zero
+    for j in range((WARM + 1) * (WARM + 1)):
+        totals[j] = small_zero
+    for j in range(ITERS * (WARM + 1)):
+        mixing[j] = small_zero
+    for j in range((INJ + 1) * (INJ + 1)):
+        dots[j] = jnp.zeros((8, toks), f32)
+    scale_out[...] = jnp.ones((toks, lanes), f32)
+
+    key_at = lax.broadcasted_iota(jnp.int32, (toks, 2 * toks), 1)
+    query_at = lax.broadcasted_iota(jnp.int32, (toks, 2 * toks), 0) + row_side * toks
+    bias[0] = jnp.where(key_at <= query_at, 0.0, -1e30).astype(f32)
+    bias[1] = jnp.zeros((toks, 2 * toks), f32)
 
     def dot_at(i, j):
         return dots[(INJ + 1) * i + j]
@@ -251,7 +271,7 @@
     def total_at(i, j):
         return totals[(WARM + 1) * i + j]
 
-    def settle(k, slot, more):
+    def settle_first(k, slot):
         total = mail_total(0)
         rate = inverse_rms(total[:1])
         scale_out[...] = by_token(rate)
@@ -272,11 +292,7 @@
             for copy in wide_copies(slot):
                 copy.start()
 
-        @pl.when(more)
-        def _():
-            for c in range(EARLY):
-                relay(c)
-
+    def settle_last(k, slot):
         @pl.when(k > 0)
         def _():
             total = jnp.broadcast_to(jnp.sum(wide_total(slot), axis=1, keepdims=True), (8, lanes))
@@ -326,7 +342,7 @@
             for j in range(ITERS):
                 inner = inner + parts_now[j] * dot_at(i, j)
             square = square + parts_now[i] * inner
-        scale_in[...] = by_token(inverse_rms(jnp.maximum(square, 0.0)))
+        return inverse_rms(jnp.maximum(square, 0.0))
 
     def remix(k):
         @pl.loop(0, blocks_of(part))
@@ -342,38 +358,52 @@
         here = kv.at[slot, owner, pl.ds(c * half, half)]
         return remote(here, here, sems[0], sems[1], "seq", target)
 
-    def up_step(slot, c, k, owner, target):
-        return kv_copy(slot, c, owner, (up_s.at[c, k], up_r.at[slot, c, k]), target)
-
-    def side_step(slot, c, k, owner):
-        return kv_copy(slot, c, owner, (side_s.at[c, k], side_r.at[slot, c, k]), row_partner)
-
-    def gathered(buffer):
-        return jnp.concatenate([buffer[f] for f in range(n)], axis=1)
-
-    def project(buffer, weights, cols):
-        return jnp.dot(gathered(buffer), weights[:, cols], preferred_element_type=f32)
-
-    def combined(cols, size):
-        total = proj[ITERS - 1, :, cols]
-        for j in range(ITERS - 1):
-            total = total + jnp.broadcast_to(coef[j][:1, :1], (toks, size)) * proj[j, :, cols]
-        return total
-
-    def wide_scale(ref, size):
-        return jnp.concatenate([ref[...]] * (size // lanes), axis=1)
+    def up_step(it, c, k, owner, target):
+        return kv_copy(it, c, owner, (up_s.at[c, k], up_r.at[it, c, k]), target)
+
+    def side_step(it, c, k, owner):
+        return kv_copy(it, c, owner, (side_s.at[c, k], side_r.at[it, c, k]), row_partner)
+
+    def norm_step(it, d, owner, target):
+        return remote(norms_out, norms.at[it, owner], norm_s.at[d], norm_r.at[it, d], "seq", target)
+
+    def share_norms(it, row):
+        norms_out[...] = everywhere(row)
+        norms[it, at_seq] = everywhere(row)
+        scale_in[...] = by_token(row)
+        for d in range(m - 1, 0, -1):
+            @pl.when(at_seq + d < m)
+            def _():
+                norm_step(it, d, at_seq, at_seq + d).start()
+
+    def project(buffer, rows, weights, cols):
+        tokens = jnp.concatenate([buffer[f, rows, :] for f in range(n)], axis=1)
+        return jnp.dot(tokens, weights[:, cols], preferred_element_type=f32)
+
+    def wide_scale(tile, size):
+        return jnp.concatenate([tile] * (size // lanes), axis=1)
 
     q_tile = span
     kv_tile = min(256, 2 * kv_cols)
 
-    def attend(slot, k):
-        owner = 2 * (level - k)
-        which = jnp.minimum(k, 1)
+    def attend(it, k):
+        which = min(k, 1)
+        pairs = []
+        for o in range(2):
+            owner = 2 * (level - k) + o
+            first = jnp.minimum(it, 1)
+            blend[o] = shares[first][:1, :1] * kv[first, owner].astype(f32)
+            for j in range(2, ITERS):
+                @pl.when(it >= j)
+                def _():
+                    blend[o] += shares[j][:1, :1] * kv[j, owner].astype(f32)
+
+            rate = by_token(norms[it, owner])
+            pairs.append((blend[o] * wide_scale(rate, 2 * kv_cols)).astype(bf16))
+        pair = jnp.concatenate(pairs, axis=0)
         for e in range(kv_local):
-            keys = kv[slot, pl.ds(owner, 2), :, e * HEAD_DIM : (e + 1) * HEAD_DIM].reshape(2 * toks, HEAD_DIM)
-            values = kv[
-                slot, pl.ds(owner, 2), :, kv_cols + e * HEAD_DIM : kv_cols + (e + 1) * HEAD_DIM
-            ].reshape(2 * toks, HEAD_DIM)
+            keys = pair[:, e * HEAD_DIM : (e + 1) * HEAD_DIM]
+            values = pair[:, kv_cols + e * HEAD_DIM : kv_cols + (e + 1) * HEAD_DIM]
             values = jnp.concatenate([values, jnp.ones((2 * toks, HEAD_DIM), bf16)], axis=1)
             asked = queries[e * group : (e + 1) * group].reshape(group * toks, HEAD_DIM)
             scores = lax.dot_general(asked, keys, (((1,), (1,)), ((), ())), preferred_element_type=f32)
@@ -417,111 +447,183 @@
         near_step(c, 0).start()
         keep[0, :, cols] = out_dot(me, c)
 
-    def arrive(slot, k):
+    def arrive(it, c, k):
         @pl.when(k <= level)
         def _():
             owner = at_seq - 2 * k
-            for c in range(HALVES):
-                up_step(slot, c, k - 1, owner, owner).wait_recv()
-
-                @pl.when(level + 1 < levels)
-                def _():
-                    up_step(slot, c, k, owner, at_seq + 2).start()
-
-                side_step(slot, c, k, owner).start()
-
-    def send_keys(it):
+            up_step(it, c, k - 1, owner, owner).wait_recv()
+
+            @pl.when(level + 1 < levels)
+            def _():
+                up_step(it, c, k, owner, at_seq + 2).start()
+
+            side_step(it, c, k, owner).start()
+
+    def all_rows():
+        return pl.ds(0, toks)
+
+    def collect(p):
+        gather_step(p, 0).wait()
+        for d in range(1, lines):
+            forward_step(p, d).wait()
+            gather_step(p, d).wait_send()
+
+    def send_keys(it, c):
+        rows = pl.ds(c * half, half) if isinstance(c, int) else pl.ds(pl.multiple_of(c * half, half), half)
+        for at in range(2 * kv_cols // kv_tile):
+            cols = pl.ds(at * kv_tile, kv_tile)
+            there = project(tok, rows, w_kv, cols) * wide_scale(scale_out[rows, :], kv_tile)
+            kv[it, at_seq, rows, cols] = (there + base_proj[rows, cols]).astype(bf16)
+
+        @pl.when(row_side == 0)
+        def _():
+            side_step(it, c, 0, at_seq).start()
+
+        @pl.when(level + 1 < levels)
+        def _():
+            up_step(it, c, 0, at_seq, at_seq + 2).start()
+
+    def ask(it, at):
+        cols = columns(at, q_tile)
+        there = project(tok, all_rows(), w_q, cols) * wide_scale(scale_out[...], q_tile)
+        proj[it, :, cols] = there + base_proj[:, pl.ds(pl.multiple_of(2 * kv_cols + at * q_tile, q_tile), q_tile)]
+        total = shares[0][:1, :1] * proj[0, :, cols]
+        for j in range(1, ITERS):
+            total = total + shares[j][:1, :1] * proj[j, :, cols]
+        asked = (total * wide_scale(scale_in[...], q_tile)).astype(bf16)
+        for h in range(q_tile // HEAD_DIM):
+            queries[at * (q_tile // HEAD_DIM) + h] = asked[:, h * HEAD_DIM : (h + 1) * HEAD_DIM]
+
+    def project_base():
+        for d in range(1, lines):
+            inj_forward(d).wait()
+        inj_step(0).wait()
+        for d in range(1, lines):
+            inj_step(d).wait_send()
+
+        @pl.loop(0, 2 * kv_cols // kv_tile)
+        def _(at):
+            cols = columns(at, kv_tile)
+            base_proj[:, cols] = project(tok_inj, all_rows(), w_kv, cols)
+
+        @pl.loop(0, head_cols // q_tile)
+        def _(at):
+            put = pl.ds(pl.multiple_of(2 * kv_cols + at * q_tile, q_tile), q_tile)
+            base_proj[:, put] = project(tok_inj, all_rows(), w_q, columns(at, q_tile))
+
+    hops = sorted(((c, k) for c in range(HALVES) for k in range(1, levels)), key=lambda one: one[0] + 3 * one[1])
+
+    def evaluate(it):
+        k = jnp.maximum(it - 1, 0)
         slot = lax.rem(it, 2)
-        k = jnp.maximum(it - 1, 0)
+        waiting = list(hops)
+        met = []
+
+        def forward(count):
+            for c, j in waiting[:count]:
+                arrive(it, c, j)
+                waiting.remove((c, j))
+                if all(other[1] != j for other in waiting):
+                    met.append(j - 1)
+
+        relay(0)
+        relay(1)
+
+        @pl.when(it > 0)
+        def _():
+            settle_first(k, slot)
+
+        @pl.when(it == 0)
+        def _():
+            loads[2].wait()
+            loads[3].wait()
+
+        collect(0)
+        collect(1)
+        send_keys(it, 0)
+        relay(2)
+
+        @pl.loop(1, HALVES)
+        def _(c):
+            collect(c + 1)
+
+            @pl.when(c + 1 < HALVES)
+            def _():
+                relay(c + 2)
+
+            send_keys(it, c)
+
+            @pl.when(c == HALVES - 2)
+            def _():
+                for one in waiting[:1]:
+                    arrive(it, *one)
+
+        del waiting[:1]
+        forward(2)
+
+        @pl.when(it > 0)
+        def _():
+            share_norms(it, settle_last(k, slot)[:1])
+            shares[0] = jnp.zeros((8, lanes), f32)
+            for j in range(1, ITERS):
+                shares[j] = coef[j - 1]
 
         @pl.when(it == 0)
         def _():
             total = mail_total(1)
             dots[(INJ + 1) * WARM + WARM] = everywhere(total[:1])
             dots[(INJ + 1) * INJ + INJ] = everywhere(total[1:2])
-            scale_in[...] = by_token(inverse_rms(total[2:3]))
-            loads[2].wait()
-            loads[3].wait()
-
-        @pl.when(it == 1)
-        def _():
-            for d in range(1, lines):
-                inj_forward(d).wait()
-            inj_step(0).wait()
-            for d in range(1, lines):
-                inj_step(d).wait_send()
-
-            @pl.loop(0, 2 * kv_cols // kv_tile)
-            def _(at):
-                cols = columns(at, kv_tile)
-                proj[ITERS - 1, :, cols] = project(tok_inj, w_kv, cols)
-
-            @pl.loop(0, head_cols // q_tile)
-            def _(at):
-                put = pl.ds(pl.multiple_of(2 * kv_cols + at * q_tile, q_tile), q_tile)
-                proj[ITERS - 1, :, put] = project(tok_inj, w_q, columns(at, q_tile))
-
-        @pl.loop(jnp.where(it > 0, EARLY, 0), CHUNKS)
-        def _(c):
-            relay(c)
-
-        @pl.loop(0, CHUNKS)
-        def _(c):
-            gather_step(c, 0).wait()
-            for d in range(1, lines):
-                forward_step(c, d).wait()
-                gather_step(c, d).wait_send()
-
-        @pl.loop(0, 2 * kv_cols // kv_tile)
-        def _(at):
-            cols = columns(at, kv_tile)
-            proj[k, :, cols] = project(tok, w_kv, cols) * wide_scale(scale_out, kv_tile)
-            kv[slot, at_seq, :, cols] = (combined(cols, kv_tile) * wide_scale(scale_in, kv_tile)).astype(bf16)
-
-        for c in range(HALVES):
-            @pl.when(row_side == 0)
-            def _():
-                side_step(slot, c, 0, at_seq).start()
-
-            @pl.when(level + 1 < levels)
-            def _():
-                up_step(slot, c, 0, at_seq, at_seq + 2).start()
-
-        @pl.when(it == 0)
-        def _():
+            share_norms(it, inverse_rms(total[2:3]))
             loads[4].wait()
             for d in range(lines):
                 inj_step(d).start()
 
-        @pl.loop(0, head_cols // q_tile)
+        q_tiles = head_cols // q_tile
+        early_hops = waiting[:q_tiles]
+
+        @pl.loop(0, q_tiles)
         def _(at):
-            put = pl.ds(pl.multiple_of(2 * kv_cols + at * q_tile, q_tile), q_tile)
-            proj[k, :, put] = project(tok, w_q, columns(at, q_tile)) * wide_scale(scale_out, q_tile)
-            asked = (combined(put, q_tile) * wide_scale(scale_in, q_tile)).astype(bf16)
-            for h in range(q_tile // HEAD_DIM):
-                queries[at * (q_tile // HEAD_DIM) + h] = asked[:, h * HEAD_DIM : (h + 1) * HEAD_DIM]
+            ask(it, at)
+            for index, one in enumerate(early_hops):
+                @pl.when(at == index)
+                def _():
+                    arrive(it, *one)
+
+        met.extend(sorted({j - 1 for c, j in early_hops if all(other[1] != j for other in waiting[q_tiles:])}))
+        del waiting[:q_tiles]
+
+        @pl.when(it > 0)
+        def _():
+            remix(k)
 
         for e in range(kv_local):
             top[e] = jnp.full(top.shape[1:], -1e30, f32)
             acc[e] = jnp.zeros(acc.shape[1:], f32)
 
-        arrive(slot, 1)
-
-    def finish_layer(it):
-        slot = lax.rem(it, 2)
-
-        @pl.loop(0, level + 1)
-        def _(k):
-            @pl.when(k > 0)
-            def _():
-                arrive(slot, k + 1)
-
-            @pl.when(k + row_side > 0)
-            def _():
-                for c in range(HALVES):
-                    side_step(slot, c, k, row_partner - 2 * k).wait_recv()
-
-            attend(slot, k)
+        def meet(k):
+            @pl.when(k <= level)
+            def _():
+                @pl.when(k + row_side > 0)
+                def _():
+                    for c in range(HALVES):
+                        side_step(it, c, k, row_partner - 2 * k).wait_recv()
+
+                for o in range(2):
+                    d = 2 * k - o + row_side
+
+                    @pl.when((d > 0) & (at_seq - d >= 0))
+                    def _():
+                        norm_step(it, d, at_seq, at_seq - d).wait_recv()
+
+                attend(it, k)
+
+        while waiting:
+            for k in met:
+                meet(k)
+            met.clear()
+            forward(1)
+        for k in met + [levels - 1]:
+            meet(k)
 
         for e in range(kv_local):
             for g in range(group):
@@ -556,6 +658,10 @@
         @pl.loop(1, CHUNKS)
         def _(c):
             own_dots(c)
+
+        @pl.when(it == 0)
+        def _():
+            project_base()
 
         for at in range(ROWS):
             sums[at] = zero_tile
@@ -591,44 +697,39 @@
 
         @pl.when(it + 1 < ITERS)
         def _():
-            for c in range(1, CHUNKS):
-                start_gather(c)
+            for p in range(1, count):
+                start_gather(p)
 
         for c in range(HALVES):
             @pl.when(row_side == 0)
             def _():
-                side_step(slot, c, 0, at_seq).wait_send()
+                side_step(it, c, 0, at_seq).wait_send()
 
             @pl.when(level + 1 < levels)
             def _():
-                up_step(slot, c, 0, at_seq, at_seq + 2).wait_send()
+                up_step(it, c, 0, at_seq, at_seq + 2).wait_send()
 
         @pl.loop(1, level + 1)
         def _(k):
             for c in range(HALVES):
-                side_step(slot, c, k, at_seq - 2 * k).wait_send()
+                side_step(it, c, k, at_seq - 2 * k).wait_send()
 
                 @pl.when(level + 1 < levels)
                 def _():
-                    up_step(slot, c, k, at_seq - 2 * k, at_seq + 2).wait_send()
-
-    @pl.loop(0, ITERS + 1)
+                    up_step(it, c, k, at_seq - 2 * k, at_seq + 2).wait_send()
+
+        for d in range(1, m):
+            @pl.when(at_seq + d < m)
+            def _():
+                norm_step(it, d, at_seq, at_seq + d).wait_send()
+
+    @pl.loop(0, ITERS)
     def _(it):
-        @pl.when(it > 0)
-        def _():
-            settle(it - 1, lax.rem(it, 2), it < ITERS)
-
-        @pl.when(it < ITERS)
-        def _():
-            send_keys(it)
-
-        @pl.when(it > 0)
-        def _():
-            remix(it - 1)
-
-        @pl.when(it < ITERS)
-        def _():
-            finish_layer(it)
+        evaluate(it)
+
+    settle_first(ITERS - 1, lax.rem(ITERS, 2))
+    settle_last(ITERS - 1, lax.rem(ITERS, 2))
+    remix(ITERS - 1)
 
 
 def on_device(injection, warm_start, gain_in, gain_out, w_query, w_key, w_value, w_out):
@@ -646,24 +747,25 @@
         vmem((w_key.shape[0], 2 * kv_cols), bf16), vmem(w_query.shape, bf16), vmem(w_out.shape, bf16),
         vmem((toks, part), bf16), vmem((toks, part), bf16),
         vmem((ITERS, toks, part), f32), vmem((toks, part), f32),
-        vmem((ITERS, toks, head_cols + 2 * kv_cols), f32),
+        vmem((ITERS, toks, head_cols), f32), vmem((toks, head_cols + 2 * kv_cols), f32),
         vmem((head_cols // HEAD_DIM, toks, HEAD_DIM), bf16),
-        vmem((2, m, toks, 2 * kv_cols), bf16),
+        vmem((ITERS, m, toks, 2 * kv_cols), bf16),
         vmem((kv_local, group * toks, 2 * HEAD_DIM), f32), vmem((kv_local, group * toks, lanes), f32),
         vmem((2, toks, 2 * toks), f32), vmem((toks, head_cols), bf16),
         vmem((lines, toks, part), f32),
         vmem((lines, toks, part), bf16), vmem((lines, toks, part), bf16),
         vmem((lines, toks, part), bf16), vmem((lines, toks, part), bf16),
-        vmem((ITERS, 8, lanes), f32), vmem((ITERS * ITERS, 8, lanes), f32),
+        vmem((ITERS, 8, lanes), f32), vmem((ITERS, 8, lanes), f32), vmem((ITERS * ITERS, 8, lanes), f32),
         vmem(((INJ + 1) * (INJ + 1), 8, toks), f32), vmem(((WARM + 1) * (WARM + 1), 8, lanes), f32),
         vmem((ITERS * (WARM + 1), 8, lanes), f32), vmem((ROWS, toks, lanes), f32),
+        vmem((8, toks), f32), vmem((ITERS, m, 8, toks), f32), vmem((2, toks, 2 * kv_cols), f32),
         vmem((toks, lanes), f32), vmem((toks, lanes), f32),
         vmem((3, 8, toks), f32), vmem((3, n, 8, toks), f32),
         vmem((8, lanes), f32), vmem((2, m, 8, lanes), f32),
-        dma((6,)), dma((CHUNKS, n)), dma((CHUNKS, n)), dma((n,)), dma((n,)),
-        dma((HALVES, m // 2)), dma((2, HALVES, m // 2)), dma((HALVES, m // 2)), dma((2, HALVES, m // 2)),
+        dma((6,)), dma((HALVES + 1, n)), dma((HALVES + 1, n)), dma((n,)), dma((n,)),
+        dma((HALVES, m // 2)), dma((ITERS, HALVES, m // 2)), dma((HALVES, m // 2)), dma((ITERS, HALVES, m // 2)),
         dma((CHUNKS, lines)), dma((CHUNKS, lines)), dma((CHUNKS, lines)), dma((CHUNKS, lines)),
-        dma((3, n)), dma((3, n)), dma((2, m)), dma((2, m)),
+        dma((3, n)), dma((3, n)), dma((2, m)), dma((2, m)), dma((m,)), dma((ITERS, m)),
     ]
     return pl.pallas_call(
         functools.partial(whole_kernel, n, m),

time: 163 us -> 155 us (0.951)
  Pallas kernels: 161 us -> 153 us
    pallas_call x1, Pallas kernels: 161 us -> 153 us  [on_device(): pl.pallas_call(functools.partial(whole_kernel, n, m), out_shape=jax.Shape...]
where the time goes in v2:
time: 155 us
  Pallas kernels  153 us (99%)
  local copies, waits for them, and re-layouts  1.97 us (1%)
    pallas_call x1, Pallas kernels, on_device(): pl.pallas_call(functools.partial(whole_kernel, n, m), out_shape=jax.Shape...  153 us

profile of v2, /device:TPU:0, one launch (start us, length us, event | category | flops | bytes accessed | tf_op | source)
XLA Modules:
  0.0 155.2 jit_solution(17927452855729104957)
XLA Ops:
  0.0 153.3 %shard_map.82 = f32[128,1280]{1,0:T(8,128)} custom-call(bf16[128,1280]{1,0:T(8,128)(2,1)} %inj_hbm.1, bf16[128,1280]{1,0:T(8,128)(2,1)} %warm_hbm.1, f32[4,1,1280]{2,1,0:T(1,128)} %bitcast.2, f32[4,1,1280]{2,1,0:T(1,128)} %bitcast.3, bf16[5120,1280]{1,0:T(8,128)(2,1)} %wq_hbm.1, bf16[5120,256]{1,0:T(8,128)(2,1)} %wk_hbm.1, bf16[5120,256]{1,0:T(8,128)(2,1)} %wv_hbm.1, ...), custom_call_target="tpu_custom_call" | custom-call | tf_op jit(solution)/shard_map/pallas_call | solution.py:770
  153.3 2.0 %copy.10 = f32[128,1280]{1,0:T(8,128)} copy(f32[128,1280]{1,0:T(8,128)} %shard_map.82) | data formatting | bytes 1310720

commit v3 on v2

--- a/solution.py
+++ b/solution.py
@@ -53,7 +53,7 @@
 
 def whole_kernel(n, m, inj_hbm, warm_hbm, gain_in, gain_out, wq_hbm, wk_hbm, wv_hbm, wo_hbm, out,
                  tok, tok_inj, w_kv, w_q, w_o, inj, warm, images, held, proj, base_proj, queries, kv,
-                 acc, top, bias, attended, keep, near_out, near, outgoing, far, coef, shares, gram, dots, totals, mixing, sums, norms_out, norms, blend,
+                 acc, top, bias, attended, keep, near_out, near, outgoing, far, coef, shares, gram, dots, totals, mixing, sums, norms_out, norms,
                  scale_out, scale_in, mail_out, mail, wide_out, wide,
                  load_sem, feat_s, feat_r, inj_s, inj_r, up_s, up_r, side_s, side_r,
                  near_s, near_r, far_s, far_r, mail_s, mail_r, wide_s, wide_r, norm_s, norm_r):
@@ -392,14 +392,11 @@
         for o in range(2):
             owner = 2 * (level - k) + o
             first = jnp.minimum(it, 1)
-            blend[o] = shares[first][:1, :1] * kv[first, owner].astype(f32)
+            mixed = shares[first][:1, :1] * kv[first, owner].astype(f32)
             for j in range(2, ITERS):
-                @pl.when(it >= j)
-                def _():
-                    blend[o] += shares[j][:1, :1] * kv[j, owner].astype(f32)
-
+                mixed = mixed + shares[j][:1, :1] * kv[jnp.minimum(j, it), owner].astype(f32)
             rate = by_token(norms[it, owner])
-            pairs.append((blend[o] * wide_scale(rate, 2 * kv_cols)).astype(bf16))
+            pairs.append((mixed * wide_scale(rate, 2 * kv_cols)).astype(bf16))
         pair = jnp.concatenate(pairs, axis=0)
         for e in range(kv_local):
             keys = pair[:, e * HEAD_DIM : (e + 1) * HEAD_DIM]
@@ -758,7 +755,7 @@
         vmem((ITERS, 8, lanes), f32), vmem((ITERS, 8, lanes), f32), vmem((ITERS * ITERS, 8, lanes), f32),
         vmem(((INJ + 1) * (INJ + 1), 8, toks), f32), vmem(((WARM + 1) * (WARM + 1), 8, lanes), f32),
         vmem((ITERS * (WARM + 1), 8, lanes), f32), vmem((ROWS, toks, lanes), f32),
-        vmem((8, toks), f32), vmem((ITERS, m, 8, toks), f32), vmem((2, toks, 2 * kv_cols), f32),
+        vmem((8, toks), f32), vmem((ITERS, m, 8, toks), f32),
         vmem((toks, lanes), f32), vmem((toks, lanes), f32),
         vmem((3, 8, toks), f32), vmem((3, n, 8, toks), f32),
         vmem((8, lanes), f32), vmem((2, m, 8, lanes), f32),

time: 155 us -> 154 us (level)
    pallas_call x1, Pallas kernels: 153 us -> 152 us  [on_device(): pl.pallas_call(functools.partial(whole_kernel, n, m), out_shape=jax.Shape...]
where the time goes in v3:
time: 154 us
  Pallas kernels  152 us (99%)
  local copies, waits for them, and re-layouts  1.97 us (1%)
    pallas_call x1, Pallas kernels, on_device(): pl.pallas_call(functools.partial(whole_kernel, n, m), out_shape=jax.Shape...  152 us

profile of v3, /device:TPU:0, one launch (start us, length us, event | category | flops | bytes accessed | tf_op | source)
XLA Modules:
  0.0 153.5 jit_solution(4406818519711424343)
XLA Ops:
  0.0 151.6 %shard_map.82 = f32[128,1280]{1,0:T(8,128)} custom-call(bf16[128,1280]{1,0:T(8,128)(2,1)} %inj_hbm.1, bf16[128,1280]{1,0:T(8,128)(2,1)} %warm_hbm.1, f32[4,1,1280]{2,1,0:T(1,128)} %bitcast.2, f32[4,1,1280]{2,1,0:T(1,128)} %bitcast.3, bf16[5120,1280]{1,0:T(8,128)(2,1)} %wq_hbm.1, bf16[5120,256]{1,0:T(8,128)(2,1)} %wk_hbm.1, bf16[5120,256]{1,0:T(8,128)(2,1)} %wv_hbm.1, ...), custom_call_target="tpu_custom_call" | custom-call | tf_op jit(solution)/shard_map/pallas_call | solution.py:767
  151.6 2.0 %copy.10 = f32[128,1280]{1,0:T(8,128)} copy(f32[128,1280]{1,0:T(8,128)} %shard_map.82) | data formatting | bytes 1310720
